TPU v7x, 8 devices: a whole 2x2x1 slice. The times are simulated.
8 devices in a mesh: batch: 1 (over z), tp: 2 (over y), sp: 4 (over x, core).
Axes of the slice: x: 2, y: 2, z: 1, core: 2. Of those that a mesh axis runs over, the one named last changes fastest.
Arguments:
- tokens: bfloat16 [8192, 2048], P(('batch', 'sp'))
- glob_pos: int32 [512], P('batch')
- rel_bias: float32 [16, 513], P('tp')
- w_query: bfloat16 [2048, 2048], P(None, 'tp')
- w_key: bfloat16 [2048, 2048], P(None, 'tp')
- w_value: bfloat16 [2048, 2048], P(None, 'tp')
- w_query_glob: bfloat16 [2048, 2048], P(None, 'tp')
- w_out: bfloat16 [2048, 2048], P('tp')
- w_up: bfloat16 [2048, 8192], P(None, 'tp')
- w_down: bfloat16 [8192, 2048], P('tp')
Outputs:
- output: bfloat16 [8192, 2048], P(('batch', 'sp'))
All inputs are finite; a program needn't handle non-finite values.
Results may differ from a plain program's by a relative error of at most 0.0114595.
Values are sent between devices in bfloat16 or wider.
A program may use at most 1 GiB of HBM per device.

v0:
```python
import jax
import jax.numpy as jnp
from jax import lax
from jax.sharding import PartitionSpec as P


def solution(mesh):
    n_seq = mesh.shape["sp"]
    to_right = [(sender, sender + 1) for sender in range(n_seq - 1)]
    to_left = [(sender + 1, sender) for sender in range(n_seq - 1)]

    def local_layer(tokens, glob_pos, rel_bias, w_query, w_key, w_value, w_query_glob, w_out, w_up, w_down):
        local_rows = tokens.shape[0]
        local_heads = rel_bias.shape[0]
        window = (rel_bias.shape[1] - 1) // 2
        local_dim = w_query.shape[1]
        head_dim = local_dim // local_heads
        num_glob = glob_pos.shape[0]
        n_blocks = local_rows // window
        seq_len = local_rows * n_seq
        score_scale = head_dim ** -0.5
        row_start = lax.axis_index("sp") * local_rows
        heads_shape = (local_rows, local_heads, head_dim)
        glob_shape = (num_glob, local_heads, head_dim)

        def project(weight):
            return jnp.dot(tokens, weight, preferred_element_type=jnp.float32).astype(jnp.bfloat16)

        q_flat = project(w_query)
        k_flat = project(w_key)
        v_flat = project(w_value)
        local_slot = glob_pos - row_start
        is_owned = (local_slot >= 0) & (local_slot < local_rows)
        safe_slot = jnp.clip(local_slot, 0, local_rows - 1)
        zero_half = jnp.zeros((), jnp.bfloat16)

        def pick_rows(source):
            return jnp.where(is_owned[:, None], jnp.take(source, safe_slot, axis=0), zero_half)

        qg_part = jnp.dot(pick_rows(tokens), w_query_glob, preferred_element_type=jnp.float32).astype(jnp.bfloat16)
        glob_rows = lax.psum(jnp.stack([qg_part, pick_rows(k_flat), pick_rows(v_flat)]), "sp")
        glob_q = glob_rows[0].reshape(glob_shape)
        glob_k = glob_rows[1].reshape(glob_shape)
        glob_v = glob_rows[2].reshape(glob_shape)

        kv_loc = jnp.stack([k_flat, v_flat]).reshape((2,) + heads_shape)
        left_halo = lax.ppermute(kv_loc[:, local_rows - window:], "sp", to_right)
        right_halo = lax.ppermute(kv_loc[:, :window], "sp", to_left)
        kv_ext = jnp.concatenate([left_halo, kv_loc, right_halo], axis=1)
        kv_blocks = kv_ext.reshape(2, n_blocks + 2, window, local_heads, head_dim)
        kv_win = jnp.concatenate([kv_blocks[:, :-2], kv_blocks[:, 1:-1], kv_blocks[:, 2:]], axis=2)
        q_blocks = q_flat.reshape(n_blocks, window, local_heads, head_dim)

        rel_offs = jnp.arange(3 * window)[None, :] - jnp.arange(window)[:, None]
        in_band = (rel_offs >= 0) & (rel_offs <= 2 * window)
        band_bias = jnp.take(rel_bias, jnp.clip(rel_offs, 0, 2 * window), axis=1)
        blk_start = row_start + jnp.arange(n_blocks) * window
        key_pos = blk_start[:, None] - window + jnp.arange(3 * window)[None, :]
        key_ok = (key_pos >= 0) & (key_pos < seq_len)
        win_mask = in_band[None, None] & key_ok[:, None, None, :]
        win_scores = jnp.einsum("cqhd,ckhd->chqk", q_blocks, kv_win[0], preferred_element_type=jnp.float32)
        win_scores = jnp.where(win_mask, win_scores * score_scale + band_bias, -jnp.inf)
        query_pos = blk_start[:, None] + jnp.arange(window)[None, :]
        far_mask = jnp.abs(query_pos[:, :, None] - glob_pos[None, None, :]) > window
        glob_scores = jnp.einsum("cqhd,ghd->chqg", q_blocks, glob_k, preferred_element_type=jnp.float32)
        glob_scores = jnp.where(far_mask[:, None], glob_scores * score_scale, -jnp.inf)
        row_max = jnp.maximum(win_scores.max(axis=-1), glob_scores.max(axis=-1))[..., None]
        win_exp = jnp.exp(win_scores - row_max)
        glob_exp = jnp.exp(glob_scores - row_max)
        soft_sum = win_exp.sum(axis=-1, keepdims=True) + glob_exp.sum(axis=-1, keepdims=True)
        win_out = jnp.einsum("chqk,ckhd->cqhd", (win_exp / soft_sum).astype(jnp.bfloat16), kv_win[1], preferred_element_type=jnp.float32)
        win_out = win_out + jnp.einsum("chqg,ghd->cqhd", (glob_exp / soft_sum).astype(jnp.bfloat16), glob_v, preferred_element_type=jnp.float32)
        win_out = win_out.astype(jnp.bfloat16).reshape(heads_shape)

        part_scores = jnp.einsum("ghd,rhd->hgr", glob_q, kv_loc[0], preferred_element_type=jnp.float32) * score_scale
        part_max = part_scores.max(axis=-1)
        part_exp = jnp.exp(part_scores - part_max[..., None])
        part_sum = part_exp.sum(axis=-1)
        part_out = jnp.einsum("hgr,rhd->ghd", part_exp.astype(jnp.bfloat16), kv_loc[1], preferred_element_type=jnp.float32)
        glob_max = lax.pmax(part_max, "sp")
        rescale = jnp.exp(part_max - glob_max)
        tot_sum, tot_out = lax.psum((part_sum * rescale, part_out * rescale.T[:, :, None]), "sp")
        glob_out = (tot_out / tot_sum.T[:, :, None]).astype(jnp.bfloat16)
        slot_rows = jnp.where(is_owned, local_slot, local_rows)
        heads_out = win_out.at[slot_rows].set(glob_out, mode="drop")

        attn_part = jnp.dot(heads_out.reshape(local_rows, local_dim), w_out, preferred_element_type=jnp.float32)
        attn_proj = lax.psum(attn_part, "tp")
        hidden = (tokens.astype(jnp.float32) + attn_proj).astype(jnp.bfloat16)
        act_vals = jax.nn.gelu(jnp.dot(hidden, w_up, preferred_element_type=jnp.float32)).astype(jnp.bfloat16)
        mlp_out = lax.psum(jnp.dot(act_vals, w_down, preferred_element_type=jnp.float32), "tp")
        return (hidden.astype(jnp.float32) + mlp_out).astype(jnp.bfloat16)

    row_spec = P(("batch", "sp"), None)
    col_spec = P(None, "tp")
    head_spec = P("tp", None)
    in_specs = (row_spec, P("batch"), head_spec, col_spec, col_spec, col_spec, col_spec, head_spec, col_spec, head_spec)
    return jax.shard_map(local_layer, mesh=mesh, in_specs=in_specs, out_specs=row_spec, check_vma=False)
```

profile of v0, /device:TPU:0, one launch (start us, length us, event | category | flops | bytes accessed | tf_op | source)
XLA Modules:
  0.0 2027.1 jit_solution(6977200074785000796)
XLA Ops:
  6.5 14.0 convolution_convert_fusion.1
  20.6 6.4 copy.78
  27.0 9.7 gather_fusion.1
  36.7 5.5 gather_fusion.2
  42.2 14.2 convolution_convert_fusion
  56.3 6.4 copy.79
  62.7 5.5 gather_fusion.3
  68.2 0.3 fusion.48
  68.5 5.2 fusion.41
  73.7 2.0 pad_maximum_fusion.1
  75.8 0.0 all-reduce.7.cloned.1.call-start
  75.8 6.7 copy.71
  82.5 6.7 copy.70
  89.3 3.2 pad_maximum_fusion.3
  92.4 1.3 collective-permute-start.1
  93.7 4.4 collective-permute-start
  98.1 0.1 compare_select_fusion
  98.2 0.8 fusion.55
  99.0 0.6 compare_select_fusion.2
  99.5 0.1 iota_add_fusion.1
  99.6 1.2 abs_compare_fusion
  100.8 11.5 convert_bitcast_fusion
  112.3 3.1 copy.104
  115.5 0.1 copy.76
  115.6 0.1 reshape.189
  115.6 0.1 broadcast_clamp_fusion
  115.8 645.2 %gather_fusion = f32[196608,8]{1,0:T(8,128)} fusion(f32[8,513]{0,1:T(8,128)S(1)} %copy.76, s32[196608]{0:T(1024)S(1)} %broadcast_clamp_fusion), kind=kCustom, calls=%fused_computation.2 | custom fusion | bytes 13369344 | tf_op jit(solution)/shard_map/jit(_take)/gather | solution.py:56
  761.0 55.5 %copy.77 = f32[256,768,8]{1,0,2:T(8,128)} copy(f32[256,768,8]{2,1,0:T(8,128)} %bitcast.5) | data formatting | bytes 12582912 | tf_op jit(solution)/shard_map/jit(_take)/gather | solution.py:56
  816.5 0.1 fusion.59
  816.6 0.1 fusion.56
  816.7 0.7 broadcast_and_fusion
  817.4 6.6 select_bitcast_fusion
  824.1 19.2 pad_maximum_fusion
  843.3 8.9 fusion.71
  852.3 9.2 copy_dynamic-update-slice_fusion.2
  861.5 9.2 copy_dynamic-update-slice_fusion.1
  870.6 9.2 copy_dynamic-update-slice_fusion
  879.9 29.3 %fusion.9 = (f32[8,8,256]{2,1,0:T(8,128)S(1)}, f32[8,8,256,768]{3,2,1,0:T(8,128)}) fusion(f32[8,256,768]{2,1,0:T(8,128)} %select_bitcast_fusion, pred[8,256,768]{2,1,0:T(8,128)(4,1)S(1)} %broadcast_and_fusion, bf16[2,8,768,8,128]{4,2,3,1,0:T(8,128)(2,1)} %copy_dynamic-update-slice_fusion, bf16[8,256,8,128]{3,2,1,0:T(8,128)(2,1)} %bitcast.95), kind=kOutput, calls=%fused_computation.22 | convolution fusion | flops 3271540736 | bytes 75038720 | tf_op jit(solution)/shard_map/cqhd,ckhd->chqk/dot_general | solution.py:61
  909.2 3.6 slice_bitcast_fusion.6
  912.8 2.3 copy.99
  915.1 1.5 copy.105
  916.6 16.6 fusion.13
  933.2 23.1 %fusion = f32[8,8,256]{2,1,0:T(8,128)S(1)} fusion(f32[8,8,256,768]{3,2,1,0:T(8,128)} %get-tuple-element.22, f32[8,8,256]{2,1,0:T(8,128)S(1)} %copy_maximum_fusion, f32[8,256,768]{2,1,0:T(8,128)} %select_bitcast_fusion, pred[8,256,768]{2,1,0:T(8,128)(4,1)S(1)} %broadcast_and_fusion), kind=kLoop, calls=%fused_computation.9 | loop fusion | flops 62898176 | bytes 58327040 | tf_op jit(solution)/shard_map/reduce_sum | solution.py:70
  956.4 14.9 fusion.10
  971.4 0.3 copy.106
  971.7 13.1 multiply_reduce_fusion
  984.8 11.9 pmax.7
  996.7 14.0 fusion.11
  1010.7 16.7 bitcast_multiply_fusion
  1027.4 0.0 all-reduce.9.cloned.1.call-start
  1027.5 18.5 fusion.17
  1046.0 34.1 %fusion.24 = bf16[8,256,8,128]{1,3,2,0:T(8,128)(2,1)} fusion(f32[8,128,8,256]{3,1,0,2:T(8,128)} %fusion.17, f32[8,8,256,768]{3,2,1,0:T(8,128)} %get-tuple-element.22, f32[8,8,256]{2,1,0:T(8,128)S(1)} %copy_add_fusion, f32[8,8,256]{2,1,0:T(8,128)S(1)} %copy_maximum_fusion, f32[8,256,768]{2,1,0:T(8,128)} %select_bitcast_fusion, ...), kind=kOutput, calls=%fused_computation.45 | convolution fusion | flops 3300917248 | bytes 83492864 | tf_op jit(solution)/shard_map/chqk,ckhd->cqhd/dot_general | solution.py:71
  1080.0 6.7 copy.89
  1086.7 10.4 psum.37
  1097.1 1.9 divide_convert_fusion.5
  1099.0 0.8 copy.92
  1099.7 47.0 %scatter_fusion = bf16[2048,8,128]{2,1,0:T(8,128)(2,1)} fusion(bf16[2048,8,128]{2,1,0:T(8,128)(2,1)} %bitcast.97, s32[512]{0:T(512)S(1)} %copy-done.7, bf16[512,8,128]{2,1,0:T(8,128)(2,1)S(1)} %copy.92), kind=kCustom, calls=%fused_computation.4 | custom fusion | bytes 3147776 | tf_op jit(solution)/shard_map/scatter | solution.py:85
  1146.8 15.1 fusion.25
  1161.9 0.0 all-reduce.11.cloned.1.call-start
  1161.9 373.0 %all-reduce.9.cloned.1.call-done = f32[2048,2048]{1,0:T(8,128)} async-done(((f32[2048,2048]{1,0:T(8,128)}), f32[2048,2048]{1,0:T(8,128)}) %all-reduce.9.cloned.1.call-update) | async-done | bytes 16777232 | tf_op jit(solution)/shard_map/psum | solution.py:88
  1534.9 46.2 %fusion.70 = f32[2048,4096]{1,0:T(8,128)} fusion(bf16[2048,4096]{1,0:T(8,128)(2,1)} %param.20, f32[2048,2048]{1,0:T(8,128)} %all-reduce.9.cloned.1.call-done, bf16[2048,2048]{1,0:T(8,128)(2,1)} %param.12), kind=kOutput, calls=%fused_computation.117 | convolution fusion | flops 34372321280 | bytes 75497472 | tf_op jit(solution)/shard_map/dot_general | solution.py:90
  1581.2 48.2 %fusion.21 = f32[2048,2048]{1,0:T(8,128)} fusion(bf16[4096,2048]{1,0:T(8,128)(2,1)} %param.21, f32[2048,4096]{1,0:T(8,128)} %fusion.70), kind=kOutput, calls=%fused_computation.36 | convolution fusion | flops 34435235840 | bytes 67108864 | tf_op jit(solution)/shard_map/dot_general | solution.py:91
  1629.4 372.7 %all-reduce.11.cloned.1.call-done = f32[2048,2048]{1,0:T(8,128)} async-done(((f32[2048,2048]{1,0:T(8,128)}), f32[2048,2048]{1,0:T(8,128)}) %all-reduce.11.cloned.1.call-update) | async-done | bytes 16777232 | tf_op jit(solution)/shard_map/psum | solution.py:91
  2002.1 18.0 add_convert_fusion
  (35 shorter events, 0.2 us)
Async XLA Ops:
  6.5 902.6 %all-reduce.5.cloned.1.call-start = ((), (), s32[]{:S(2)}) async-start(), calls=%async_computation | async-start | bytes 6291456 | tf_op jit(solution)/shard_map/psum | solution.py:41
  6.5 20.4 %copy-start.6 = (s32[512]{0:T(512)S(1)}, s32[512]{0:T(512)}, u32[]{:S(2)}) copy-start(s32[512]{0:T(512)} %param.13) | copy-start | bytes 6148
  75.8 1021.3 %all-reduce.7.cloned.1.call-start = ((), (), s32[]{:S(2)}) async-start(), calls=%async_computation.1 | async-start | bytes 4194304 | tf_op jit(solution)/shard_map/psum | solution.py:82
  89.3 11.5 copy-start.8
  92.4 731.6 %collective-permute-start.1 = (bf16[2,256,8,128]{3,2,1,0:T(8,128)(2,1)}, bf16[2,256,8,128]{3,2,1,0:T(8,128)(2,1)}, u32[]{:S(2)}, u32[]{:S(2)}) collective-permute-start(bf16[2,256,8,128]{3,2,1,0:T(8,128)(2,1)} %get-tuple-element.12), channel_id=1, source_target_pairs={{1,0},{2,1},{3,2},{5,4},{6,5},{7,6}} | collective-permute-start | bytes 3145736 | tf_op jit(solution)/shard_map/ppermute | solution.py:48
  93.7 730.4 %collective-permute-start = (bf16[2,256,8,128]{3,2,1,0:T(8,128)(2,1)}, bf16[2,256,8,128]{3,2,1,0:T(8,128)(2,1)}, u32[]{:S(2)}, u32[]{:S(2)}) collective-permute-start(bf16[2,256,8,128]{3,2,1,0:T(8,128)(2,1)} %get-tuple-element.11), channel_id=1, source_target_pairs={{0,1},{1,2},{2,3},{4,5},{5,6},{6,7}} | collective-permute-start | bytes 3145736 | tf_op jit(solution)/shard_map/ppermute | solution.py:47
  100.8 14.7 copy-start.5
  761.0 56.4 %copy-start.4 = (pred[256,768]{1,0:T(8,128)(4,1)S(1)}, pred[256,768]{1,0:T(8,128)(4,1)}, u32[]{:S(2)}) copy-start(pred[256,768]{1,0:T(8,128)(4,1)} %fusion.55) | copy-start | bytes 589828
  816.5 7.5 copy-start.1
  816.5 7.6 copy-start.2
  956.3 15.0 copy-start.3
  956.4 15.3 copy-start
  1027.4 507.5 %all-reduce.9.cloned.1.call-start = ((), (), s32[]{:S(2)}) async-start(), calls=%async_computation.2 | async-start | bytes 33554432 | tf_op jit(solution)/shard_map/psum | solution.py:88
  1080.0 19.7 copy-start.7
  1161.9 840.2 %all-reduce.11.cloned.1.call-start = ((), (), s32[]{:S(2)}) async-start(), calls=%async_computation.3 | async-start | bytes 33554432 | tf_op jit(solution)/shard_map/psum | solution.py:91
Sparse Core Ops, SparseCore 0:
  75.9 70.4 all-reduce.4
  1027.6 46.4 all-reduce.6
  1162.0 372.9 all-reduce.8
  1629.5 372.4 all-reduce.10
where the time goes:
time: 2040 us; the launch traced here: 2030 us
  local copies, waits for them, and re-layouts  850 us (42%)
  waiting for transfers between devices  746 us (37%)
  matrix products  283 us (14%)
  other arithmetic  107 us (5%)
  blocking collectives  22.3 us (1%)
    gather x2, local copies, waits for them, and re-layouts, local_layer(): band_bias = jnp.take(rel_bias, jnp.clip(rel_offs, 0, 2 * window), axis=1)  701 us
    psum x1, waiting for transfers between devices, local_layer(): attn_proj = lax.psum(attn_part, 'tp')  373 us
    psum x1, waiting for transfers between devices, local_layer(): lax.psum(jnp.dot(act_vals, w_down, preferred_element_type=jnp.float32), '...  373 us
    dot_general x1, matrix products, local_layer(): jnp.dot(act_vals, w_down, preferred_element_type=jnp.float32)  48.2 us
    scatter x1, local copies, waits for them, and re-layouts, local_layer(): heads_out = win_out.at[slot_rows].set(glob_out, mode='drop')  47 us
    dot_general x1, matrix products, local_layer(): jnp.dot(hidden, w_up, preferred_element_type=jnp.float32)  46.2 us
  transfers between devices with their start and end apart: 6, of which 2 were waited for; matrix products, arithmetic and copies ran while one was open for 44% of the time, Pallas kernels for 0%

commit v1 on v0

v1 whole, which is shorter than its diff:
```python
import functools
import math

import jax
import jax.numpy as jnp
from jax import lax
from jax.experimental import pallas as pl
from jax.experimental.pallas import tpu as pltpu
from jax.sharding import PartitionSpec as P


LOG2E = math.log2(math.e)
LANES = 128
F32 = jnp.float32
BF16 = jnp.bfloat16
NEG = float("-inf")


def dot_nt(lhs, rhs):
    return lax.dot_general(lhs, rhs, (((1,), (1,)), ((), ())), preferred_element_type=F32)


def window_kernel(q_blk, window, seq_len, half_ref, q_ref, k_ref, v_ref, kl_ref, vl_ref, kr_ref, vr_ref,
                  kg_ref, vg_ref, rel_ref, gp_ref, o_ref, k_buf, v_buf, bias, far):
    rows = q_ref.shape[0]
    span = q_blk + 2 * window
    n_blk = rows // q_blk
    local_rows = k_ref.shape[0]
    scale = q_ref.shape[1] ** -0.5 * LOG2E
    row_start = half_ref[1] + half_ref[0] * rows
    sub_start = half_ref[0] * rows

    @pl.when(pl.program_id(0) == 0)
    def _():
        for blk in range(n_blk):
            pos = row_start + blk * q_blk + lax.broadcasted_iota(jnp.int32, (q_blk, far.shape[1]), 0)
            far[pl.ds(blk * q_blk, q_blk), :] = jnp.where(jnp.abs(pos - gp_ref[...]) > window, 0.0, NEG)

    k_buf[pl.ds(0, window), :] = kl_ref[...]
    k_buf[pl.ds(window, local_rows), :] = k_ref[...]
    k_buf[pl.ds(window + local_rows, window), :] = kr_ref[...]
    v_buf[pl.ds(0, window), :] = vl_ref[...]
    v_buf[pl.ds(window, local_rows), :] = v_ref[...]
    v_buf[pl.ds(window + local_rows, window), :] = vr_ref[...]
    base = pltpu.roll(jnp.broadcast_to(rel_ref[0], (q_blk, span)), 0, 1, stride=1, stride_axis=0)
    for blk in range(n_blk):
        key_pos = row_start + blk * q_blk - window + lax.broadcasted_iota(jnp.int32, (1, span), 1)
        ok = (key_pos >= 0) & (key_pos < seq_len)
        edge = blk * q_blk < window or (blk + 1) * q_blk + window > rows
        if edge:
            slot = 1 + (blk if blk * q_blk < window else blk - n_blk + 2 * (window // q_blk))
            bias[slot] = base + jnp.where(ok, 0.0, NEG)
    bias[0] = base

    def step(blk, slot):
        start = blk * q_blk if isinstance(blk, int) else pl.multiple_of(blk * q_blk, q_blk)
        q = q_ref[pl.ds(start, q_blk), :]
        key_start = pl.multiple_of(sub_start + start, LANES)
        win = dot_nt(q, k_buf[pl.ds(key_start, span), :]) * scale + bias[slot]
        glb = dot_nt(q, kg_ref[...]) * scale + far[pl.ds(start, q_blk), :]
        top = jnp.maximum(win.max(axis=-1, keepdims=True), glb.max(axis=-1, keepdims=True))
        win = jnp.exp2(win - top)
        glb = jnp.exp2(glb - top)
        inv = 1.0 / (win.sum(axis=-1, keepdims=True) + glb.sum(axis=-1, keepdims=True))
        out = jnp.dot((win * inv).astype(BF16), v_buf[pl.ds(key_start, span), :], preferred_element_type=F32)
        out = out + jnp.dot((glb * inv).astype(BF16), vg_ref[...], preferred_element_type=F32)
        o_ref[pl.ds(start, q_blk), :] = out.astype(BF16)

    for blk in range(n_blk):
        left = blk * q_blk < window
        right = (blk + 1) * q_blk + window > rows
        step(blk, 1 + blk if left else 1 + blk - n_blk + 2 * (window // q_blk) if right else 0)


def window_attention(info, q, k, v, kl, vl, kr, vr, kg, vg, rel, gp, seq_len, window, q_blk, halves):
    local_rows, width = q.shape
    heads = width // LANES
    rows = local_rows // halves
    span = q_blk + 2 * window
    num_glob = kg.shape[0]

    def whole(n):
        return pl.BlockSpec((n, LANES), lambda h, s: (0, h))

    grid_spec = pltpu.PrefetchScalarGridSpec(
        num_scalar_prefetch=1,
        grid=(heads,),
        in_specs=[
            pl.BlockSpec((rows, LANES), lambda h, s: (s[0], h)),
            whole(local_rows), whole(local_rows),
            whole(window), whole(window), whole(window), whole(window),
            whole(num_glob), whole(num_glob),
            pl.BlockSpec((1, 1, span), lambda h, s: (h, 0, 0)),
            pl.BlockSpec((1, num_glob), lambda h, s: (0, 0)),
        ],
        out_specs=pl.BlockSpec((rows, LANES), lambda h, s: (0, h)),
        scratch_shapes=[
            pltpu.VMEM((local_rows + 2 * window, LANES), BF16),
            pltpu.VMEM((local_rows + 2 * window, LANES), BF16),
            pltpu.VMEM((1 + 2 * (window // q_blk), q_blk, span), F32),
            pltpu.VMEM((rows, num_glob), F32),
        ],
    )
    elems = heads * rows * (span + num_glob)
    return pl.pallas_call(
        functools.partial(window_kernel, q_blk, window, seq_len),
        grid_spec=grid_spec,
        out_shape=jax.ShapeDtypeStruct((rows, width), BF16),
        compiler_params=pltpu.CompilerParams(dimension_semantics=("arbitrary",)),
        cost_estimate=pl.CostEstimate(flops=elems * LANES * 4 * 2, bytes_accessed=4 * 2 * local_rows * width,
                                      transcendentals=elems),
        name="window_attention",
    )(info, q, k, v, kl, vl, kr, vr, kg, vg, rel, gp)


def global_kernel(g_blk, q_ref, k_ref, v_ref, o_ref):
    scale = q_ref.shape[1] ** -0.5 * LOG2E
    head = pl.program_id(0)
    width = o_ref.shape[1] - LANES
    col = pl.ds(pl.multiple_of(head * LANES, LANES), LANES)
    stat = pl.ds(width, LANES)
    for start in range(0, q_ref.shape[0], g_blk):
        rows = pl.ds(start, g_blk)
        s = dot_nt(q_ref[rows, :], k_ref[...]) * scale
        top = s.max(axis=-1, keepdims=True)
        p = jnp.exp2(s - top)
        tot = p.sum(axis=-1, keepdims=True)
        o_ref[rows, col] = jnp.dot(p.astype(BF16), v_ref[...], preferred_element_type=F32)
        lane = lax.broadcasted_iota(jnp.int32, (g_blk, LANES), 1)
        old = jnp.where(head == 0, 0.0, o_ref[rows, stat])
        o_ref[rows, stat] = jnp.where(lane == head, top, jnp.where(lane == head + LANES // 2, tot, old))


def global_partial(q, k, v, g_blk):
    num_glob, width = q.shape
    heads = width // LANES
    rows = k.shape[0]
    elems = heads * rows * num_glob
    col = lambda n: pl.BlockSpec((n, LANES), lambda h: (0, h))
    return pl.pallas_call(
        functools.partial(global_kernel, g_blk),
        grid=(heads,),
        in_specs=[col(num_glob), col(rows), col(rows)],
        out_specs=pl.BlockSpec((num_glob, width + LANES), lambda h: (0, 0)),
        out_shape=jax.ShapeDtypeStruct((num_glob, width + LANES), F32),
        compiler_params=pltpu.CompilerParams(dimension_semantics=("arbitrary",)),
        cost_estimate=pl.CostEstimate(flops=elems * LANES * 4 * 2, bytes_accessed=4 * rows * width,
                                      transcendentals=elems),
        name="global_partial",
    )(q, k, v)


def solution(mesh):
    n_seq = mesh.shape["sp"]
    n_tp = mesh.shape["tp"]
    to_right = [(sender, sender + 1) for sender in range(n_seq - 1)]
    to_left = [(sender + 1, sender) for sender in range(n_seq - 1)]
    swap_tp = [(0, 1), (1, 0)]
    swap_core = [(i, i ^ 1) for i in range(n_seq)]
    swap_x = [(i, i ^ 2) for i in range(n_seq)]

    def local_layer(tokens, glob_pos, rel_bias, w_query, w_key, w_value, w_query_glob, w_out, w_up, w_down):
        local_rows, model = tokens.shape
        local_heads = rel_bias.shape[0]
        window = (rel_bias.shape[1] - 1) // 2
        local_dim = w_query.shape[1]
        num_glob = glob_pos.shape[0]
        seq_len = local_rows * n_seq
        tp = lax.axis_index("tp")
        sp = lax.axis_index("sp")
        core = sp % 2
        xpos = sp // 2
        row_start = sp * local_rows
        rows = local_rows // n_tp
        q_blk = 128

        def tp_swap(value):
            return lax.ppermute(value, "tp", swap_tp)

        def sp_swap(value, perm):
            return lax.ppermute(value, "sp", perm)

        def dot(lhs, rhs):
            return jnp.dot(lhs, rhs, preferred_element_type=F32)

        def project(lhs, rhs):
            return dot(lhs, rhs).astype(BF16)

        def quarter(weight, parts):
            step = weight.shape[0] // n_seq
            width = weight.shape[1] // parts
            return [tp_swap(lax.dynamic_slice(weight, (sp * step, i * width), (step, width)))
                    for i in range(parts)]

        def spread(value):
            return lax.all_gather(value, "sp", axis=0, tiled=True)

        def halves(value, bit):
            half = value.shape[0] // 2
            return (lax.dynamic_slice_in_dim(value, bit * half, half, 0),
                    lax.dynamic_slice_in_dim(value, (1 - bit) * half, half, 0))

        step = w_out.shape[0] // n_seq
        out_q = tp_swap(lax.dynamic_slice_in_dim(w_out, sp * step, step, 0))
        up_q = quarter(w_up, 2)
        down_q = quarter(w_down, 4)

        local_pos = glob_pos - row_start
        pick = (local_pos[:, None] == jnp.arange(local_rows)[None, :]).astype(BF16)
        x_part = project(pick, tokens)
        keep, give = halves(x_part, core)
        keep = keep + sp_swap(give, swap_core)
        keep = keep + sp_swap(keep, swap_x)
        got = sp_swap(keep, swap_core)
        x_glob = jnp.concatenate([jnp.where(core == 0, keep, got), jnp.where(core == 0, got, keep)])

        k_loc = project(tokens, w_key)
        v_loc = project(tokens, w_value)
        kv_l = sp_swap(jnp.stack([k_loc[local_rows - window:], v_loc[local_rows - window:]]), to_right)
        kv_r = sp_swap(jnp.stack([k_loc[:window], v_loc[:window]]), to_left)
        q_loc = project(tokens, w_query)
        qg = project(x_glob, w_query_glob)
        kg = project(x_glob, w_key)
        vg = project(x_glob, w_value)

        state = global_partial(qg, k_loc, v_loc, 128)

        def merge(mine, other):
            top_a, top_b = mine[:, local_dim:local_dim + local_heads], other[:, local_dim:local_dim + local_heads]
            at = local_dim + LANES // 2
            tot_a, tot_b = mine[:, at:at + local_heads], other[:, at:at + local_heads]
            best = jnp.maximum(top_a, top_b)
            fac_a = jnp.exp2(top_a - best)
            fac_b = jnp.exp2(top_b - best)

            def wide(fac):
                return jnp.repeat(fac, LANES, axis=1)

            acc = mine[:, :local_dim] * wide(fac_a) + other[:, :local_dim] * wide(fac_b)
            return acc, best, tot_a * fac_a + tot_b * fac_b

        keep, give = halves(state, core)
        acc, top, tot = merge(keep, sp_swap(give, swap_core))
        fill = jnp.zeros((acc.shape[0], LANES // 2 - local_heads), F32)
        state = jnp.concatenate([acc, top, fill, tot, fill], axis=1)
        keep, give = halves(state, xpos)
        acc, _, tot = merge(keep, sp_swap(give, swap_x))
        g_mine = (acc / jnp.repeat(tot, LANES, axis=1)).astype(BF16)
        g_pair = jnp.concatenate([g_mine, tp_swap(g_mine)], axis=1)
        g_half = jnp.concatenate([g_pair, sp_swap(g_pair, swap_x)])
        g_all = jnp.concatenate([g_half, sp_swap(g_half, swap_core)])
        part = num_glob // n_seq
        order = [core * 2 + xpos, core * 2 + 1 - xpos, (1 - core) * 2 + xpos, (1 - core) * 2 + 1 - xpos]
        gp_order = jnp.concatenate([lax.dynamic_slice_in_dim(glob_pos, i * part, part) for i in order])

        span = q_blk + 2 * window
        rel = jnp.concatenate([rel_bias * LOG2E, jnp.full((local_heads, span - rel_bias.shape[1]), NEG, F32)], axis=1)
        rel = rel[:, None, :]
        gp = glob_pos[None, :]

        def attend(unit, parts):
            info = jnp.stack([unit, row_start]).astype(jnp.int32)
            return window_attention(info, q_loc, k_loc, v_loc, kv_l[0], kv_l[1], kv_r[0], kv_r[1], kg, vg, rel, gp,
                                    seq_len, window, q_blk, parts)

        o_give = attend(1 - tp, n_tp)
        o_other = tp_swap(o_give)
        o_own = jnp.concatenate([attend(2 * tp, 2 * n_tp), attend(2 * tp + 1, 2 * n_tp)])

        my_pos = row_start + tp * rows + jnp.arange(rows)
        place = my_pos[:, None] == gp_order[None, :]
        is_glob = place.any(axis=1)[:, None]
        place = place.astype(BF16)
        o_own = jnp.where(is_glob, dot(place, g_all[:, :local_dim]).astype(BF16), o_own)
        o_other = jnp.where(is_glob, dot(place, g_all[:, local_dim:]).astype(BF16), o_other)

        x_mine = lax.dynamic_slice_in_dim(tokens, tp * rows, rows, 0)
        proj = dot(o_own, w_out)
        hidden = (x_mine.astype(F32) + (proj + dot(o_other, spread(out_q)))).astype(BF16)
        acts = [jax.nn.gelu(dot(hidden, w_up)).astype(BF16)]
        for piece in up_q:
            acts.append(jax.nn.gelu(dot(hidden, spread(piece))).astype(BF16))
        width = acts[1].shape[1]
        cols = model // len(down_q)
        out = jnp.zeros((local_rows, model), BF16)
        for i, piece in enumerate(down_q):
            sl = slice(i * cols, (i + 1) * cols)
            w_piece = spread(piece)
            total = dot(acts[0], w_down[:, sl])
            for j in range(len(up_q)):
                total = total + dot(acts[1 + j], w_piece[j * width:(j + 1) * width])
            mine = (hidden[:, sl].astype(F32) + total).astype(BF16)
            out = lax.dynamic_update_slice(out, mine, (tp * rows, i * cols))
            out = lax.dynamic_update_slice(out, tp_swap(mine), ((1 - tp) * rows, i * cols))
        return out

    row_spec = P(("batch", "sp"), None)
    col_spec = P(None, "tp")
    head_spec = P("tp", None)
    in_specs = (row_spec, P("batch"), head_spec, col_spec, col_spec, col_spec, col_spec, head_spec, col_spec, head_spec)
    return jax.shard_map(local_layer, mesh=mesh, in_specs=in_specs, out_specs=row_spec, check_vma=False)
```

time: 2040 us -> 672 us (0.33)
  local copies, waits for them, and re-layouts: 850 us -> 40.8 us
  waiting for transfers between devices: 746 us -> 258 us
  Pallas kernels: 0 us -> 101 us
  other arithmetic: 107 us -> 13.4 us
  matrix products: 283 us -> 209 us
  blocking collectives: 22.3 us -> 0 us
  starting transfers between devices: 5.76 us -> 27 us
    psum x4 -> x0, waiting for transfers between devices: 746 us -> none  [the longest x1 373 us: local_layer(): attn_proj = lax.psum(attn_part, 'tp')]
    gather x5 -> x0, local copies, waits for them, and re-layouts: 721 us -> none  [the longest x2 701 us: local_layer(): band_bias = jnp.take(rel_bias, jnp.clip(rel_offs, 0, 2 * window), axis=1)]
    ppermute x2 -> x22, waiting for transfers between devices: 0.01 us -> 258 us  [the longest x13 199 us: tp_swap(): return lax.ppermute(value, 'tp', swap_tp)]
    pallas_call x0 -> x4, Pallas kernels: none -> 101 us  [the longest x3 80.2 us: window_attention(): pl.pallas_call(functools.partial(window_kernel, q_blk, window, seq_len),...]
    dot_general x13 -> x24, matrix products: 283 us -> 209 us  [dot(): return jnp.dot(lhs, rhs, preferred_element_type=F32)]
    reduce_sum x3 -> x0, other arithmetic: 52.1 us -> none  [the longest x1 23.1 us: local_layer(): win_exp.sum(axis=-1, keepdims=True) + glob_exp.sum(axis=-1, keepdims=True)]
    scatter x1 -> x0, local copies, waits for them, and re-layouts: 47 us -> none  [local_layer(): heads_out = win_out.at[slot_rows].set(glob_out, mode='drop')]
    ppermute x2 -> x22, starting transfers between devices: 5.64 us -> 26.8 us  [the longest x13 18.4 us: tp_swap(): return lax.ppermute(value, 'tp', swap_tp)]
  transfers between devices with their start and end apart: 6 -> 29, of which waited for: 2 -> 13; matrix products, arithmetic and copies ran while one was open for 44% -> 37% of each run, Pallas kernels for 0% -> 15%
where the time goes in v1:
time: 672 us; the launch traced here: 663 us
  waiting for transfers between devices  258 us (38%)
  matrix products  209 us (31%)
  Pallas kernels  101 us (15%)
  local copies, waits for them, and re-layouts  40.8 us (6%)
  starting transfers between devices  27 us (4%)
  between operations  14.2 us (2%)
  other arithmetic  13.4 us (2%)
    dot_general x24, matrix products, dot(): return jnp.dot(lhs, rhs, preferred_element_type=F32)  209 us
    ppermute x13, waiting for transfers between devices, tp_swap(): return lax.ppermute(value, 'tp', swap_tp)  199 us
    pallas_call x3, Pallas kernels, window_attention(): pl.pallas_call(functools.partial(window_kernel, q_blk, window, seq_len),...  80.2 us
    ppermute x9, waiting for transfers between devices, sp_swap(): return lax.ppermute(value, 'sp', perm)  58.5 us
    pallas_call x1, Pallas kernels, global_partial(): pl.pallas_call(functools.partial(global_kernel, g_blk), grid=(heads,), in...  20.7 us
    ppermute x13, starting transfers between devices, tp_swap(): return lax.ppermute(value, 'tp', swap_tp)  18.4 us
  transfers between devices with their start and end apart: 29, of which 13 were waited for; matrix products, arithmetic and copies ran while one was open for 37% of the time, Pallas kernels for 15%

profile of v1, /device:TPU:0, one launch (start us, length us, event | category | flops | bytes accessed | tf_op | source)
XLA Modules:
  0.0 663.2 jit_solution(859274210549504896)
XLA Ops:
  7.9 3.4 collective-permute-start.11
  11.2 23.2 %collective-permute-done.11 = bf16[256,2048]{1,0:T(8,128)(2,1)S(1)} collective-permute-done((bf16[256,2048]{1,0:T(8,128)(2,1)S(1)}, bf16[256,2048]{1,0:T(8,128)(2,1)S(1)}, u32[]{:S(2)}, u32[]{:S(2)}) %collective-permute-start.11) | collective-permute-done | bytes 1048608 | tf_op jit(solution)/shard_map/ppermute | solution.py:178
  35.4 4.1 constant_dynamic-slice_fusion.9
  39.5 1.7 collective-permute-start.12
  41.2 45.1 %collective-permute-done.12 = bf16[512,2048]{1,0:T(8,128)(2,1)S(1)} collective-permute-done((bf16[512,2048]{1,0:T(8,128)(2,1)S(1)}, bf16[512,2048]{1,0:T(8,128)(2,1)S(1)}, u32[]{:S(2)}, u32[]{:S(2)}) %collective-permute-start.12) | collective-permute-done | bytes 2097184 | tf_op jit(solution)/shard_map/ppermute | solution.py:178
  87.7 1.5 collective-permute-start.14
  89.2 44.7 %collective-permute-done.14 = bf16[512,2048]{1,0:T(8,128)(2,1)S(1)} collective-permute-done((bf16[512,2048]{1,0:T(8,128)(2,1)}, bf16[512,2048]{1,0:T(8,128)(2,1)S(1)}, u32[]{:S(2)}, u32[]{:S(2)}) %collective-permute-start.14) | collective-permute-done | bytes 2097184 | tf_op jit(solution)/shard_map/ppermute | solution.py:178
  135.2 3.8 constant_dynamic-slice_fusion.6
  140.2 21.5 %collective-permute-done.13 = bf16[1024,512]{1,0:T(8,128)(2,1)S(1)} collective-permute-done((bf16[1024,512]{1,0:T(8,128)(2,1)S(1)}, bf16[1024,512]{1,0:T(8,128)(2,1)S(1)}, u32[]{:S(2)}, u32[]{:S(2)}) %collective-permute-start.13) | collective-permute-done | bytes 1048608 | tf_op jit(solution)/shard_map/ppermute | solution.py:178
  163.8 8.2 %fusion.37 = bf16[512,2048]{1,0:T(8,128)(2,1)S(1)} fusion(bf16[2048,2048]{1,0:T(8,128)(2,1)} %param.10, s32[512]{0:T(512)S(1)} %broadcast_subtract_fusion), kind=kOutput, calls=%fused_computation.46 | convolution fusion | flops 4297064448 | bytes 10487808 | tf_op jit(solution)/shard_map/dot_general | solution.py:184
  173.0 13.1 %collective-permute-done.16 = bf16[1024,512]{1,0:T(8,128)(2,1)} collective-permute-done((bf16[1024,512]{1,0:T(8,128)(2,1)}, bf16[1024,512]{1,0:T(8,128)(2,1)}, u32[]{:S(2)}, u32[]{:S(2)}) %collective-permute-start.16) | collective-permute-done | bytes 1048608 | tf_op jit(solution)/shard_map/ppermute | solution.py:178
  187.1 1.8 dynamic-slice_add_fusion
  188.9 1.5 collective-permute-start.1
  190.4 13.2 %convolution_convert_fusion.1.v_ref = bf16[2048,1024]{1,0:T(8,128)(2,1)S(1)} fusion(bf16[2048,2048]{1,0:T(8,128)(2,1)} %param.10, bf16[2048,1024]{1,0:T(8,128)(2,1)} %param.15), kind=kOutput, calls=%fused_computation.39 | convolution fusion | flops 8592031744 | bytes 16777216 | tf_op jit(solution)/shard_map/dot_general | solution.py:184
  203.6 18.3 %collective-permute-done.1 = bf16[256,2048]{1,0:T(8,128)(2,1)S(1)} collective-permute-done((bf16[256,2048]{1,0:T(8,128)(2,1)S(1)}, bf16[256,2048]{1,0:T(8,128)(2,1)S(1)}, u32[]{:S(2)}, u32[]{:S(2)}) %collective-permute-start.1) | collective-permute-done | bytes 1048608 | tf_op jit(solution)/shard_map/ppermute | solution.py:181
  222.4 9.1 %convolution_convert_fusion.2.k_ref = bf16[2048,1024]{1,0:T(8,128)(2,1)S(1)} fusion(bf16[2048,2048]{1,0:T(8,128)(2,1)S(1)} %bitcast.87, bf16[2048,1024]{1,0:T(8,128)(2,1)S(1)} %copy-done.14), kind=kOutput, calls=%fused_computation.40 | convolution fusion | flops 8592031744 | bytes 16777216 | tf_op jit(solution)/shard_map/dot_general | solution.py:184
  236.4 4.4 collective-permute-start.8
  240.8 1.5 collective-permute-start.20
  242.3 1.5 broadcast_select_fusion.1
  245.0 3.3 convolution_convert_fusion.5.q_ref
  248.4 20.7 %global_partial.1 = f32[512,1152]{1,0:T(8,128)} custom-call(bf16[512,1024]{1,0:T(8,128)(2,1)} %convolution_convert_fusion.5.q_ref, bf16[2048,1024]{1,0:T(8,128)(2,1)} %copy-done.9, bf16[2048,1024]{1,0:T(8,128)(2,1)} %copy-done.8), custom_call_target="tpu_custom_call" | custom-call | flops 8589934592 | bytes 8388608 | tf_op jit(solution)/shard_map/global_partial/pallas_call | solution.py:140
  269.1 1.3 constant_dynamic-slice_fusion.4
  270.8 13.8 %convolution_convert_fusion.q_ref = bf16[2048,1024]{1,0:T(8,128)(2,1)} fusion(bf16[2048,2048]{1,0:T(8,128)(2,1)} %param.10, bf16[2048,1024]{1,0:T(8,128)(2,1)} %param.13), kind=kOutput, calls=%fused_computation.38 | convolution fusion | flops 8592031744 | bytes 16777216 | tf_op jit(solution)/shard_map/dot_general | solution.py:184
  286.5 1.7 fusion.94
  288.9 2.0 fusion.79
  290.8 1.3 concatenate.27
  293.2 2.4 slice_bitcast_fusion
  295.6 2.4 slice_bitcast_fusion.4
  298.0 22.9 %collective-permute-done.4 = f32[128,1152]{1,0:T(8,128)S(1)} collective-permute-done((f32[128,1152]{1,0:T(8,128)S(1)}, f32[128,1152]{1,0:T(8,128)S(1)}, u32[]{:S(2)}, u32[]{:S(2)}) %collective-permute-start.4) | collective-permute-done | bytes 589856 | tf_op jit(solution)/shard_map/ppermute | solution.py:181
  322.7 3.3 convolution_convert_fusion.3.vg_ref
  326.0 4.0 collective-permute-done.5
  330.5 3.3 convolution_convert_fusion.4.kg_ref
  333.8 17.3 %collective-permute-done.6 = bf16[128,2048]{1,0:T(8,128)(2,1)S(1)} collective-permute-done((bf16[128,2048]{1,0:T(8,128)(2,1)S(1)}, bf16[128,2048]{1,0:T(8,128)(2,1)S(1)}, u32[]{:S(2)}, u32[]{:S(2)}) %collective-permute-start.6) | collective-permute-done | bytes 524320 | tf_op jit(solution)/shard_map/ppermute | solution.py:181
  351.2 37.2 %window_attention.5 = bf16[1024,1024]{1,0:T(8,128)(2,1)} custom-call(s32[2]{0:T(128)} %pad_add_fusion.3.half_ref, bf16[2048,1024]{1,0:T(8,128)(2,1)} %convolution_convert_fusion.q_ref, bf16[2048,1024]{1,0:T(8,128)(2,1)} %copy-done.9, bf16[2048,1024]{1,0:T(8,128)(2,1)} %copy-done.8, bf16[256,1024]{1,0:T(8,128)(2,1)} %get-tuple-element.27.kl_ref, ...), custom_call_target="tpu_custom_call" | custom-call | flops 9663676416 | bytes 16777216 | tf_op jit(solution)/shard_map/window_attention/pallas_call | solution.py:105
  388.4 21.4 %window_attention.3 = bf16[512,1024]{1,0:T(8,128)(2,1)} custom-call(s32[2]{0:T(128)} %get-tuple-element.40.half_ref, bf16[2048,1024]{1,0:T(8,128)(2,1)} %convolution_convert_fusion.q_ref, bf16[2048,1024]{1,0:T(8,128)(2,1)} %copy-done.9, bf16[2048,1024]{1,0:T(8,128)(2,1)} %copy-done.8, bf16[256,1024]{1,0:T(8,128)(2,1)} %get-tuple-element.27.kl_ref, ...), custom_call_target="tpu_custom_call" | custom-call | flops 4831838208 | bytes 16777216 | tf_op jit(solution)/shard_map/window_attention/pallas_call | solution.py:105
  409.8 21.6 %window_attention.4 = bf16[512,1024]{1,0:T(8,128)(2,1)} custom-call(s32[2]{0:T(128)} %get-tuple-element.41.half_ref, bf16[2048,1024]{1,0:T(8,128)(2,1)} %convolution_convert_fusion.q_ref, bf16[2048,1024]{1,0:T(8,128)(2,1)} %copy-done.9, bf16[2048,1024]{1,0:T(8,128)(2,1)} %copy-done.8, bf16[256,1024]{1,0:T(8,128)(2,1)} %get-tuple-element.27.kl_ref, ...), custom_call_target="tpu_custom_call" | custom-call | flops 4831838208 | bytes 16777216 | tf_op jit(solution)/shard_map/window_attention/pallas_call | solution.py:105
  431.4 1.4 pad_maximum_fusion.1
  432.7 11.9 %fusion.54 = f32[1024,2048]{1,0:T(8,128)} fusion(bf16[1024,2048]{1,0:T(8,128)(2,1)} %param.17, bf16[512,1024]{1,0:T(8,128)(2,1)} %window_attention.4, bf16[512,1024]{1,0:T(8,128)(2,1)} %window_attention.3, pred[1024]{0:T(1024)(128)(4,1)S(1)} %compare_reduce_fusion, bf16[512,2048]{1,0:T(8,128)(2,1)S(1)} %pad_maximum_fusion.1, s32[512]{0:T(512)S(1)} %pad_add_fusion, ...), kind=kOutput, calls=%fused_computation.66 | convolution fusion | flops 5375524864 | bytes 15735808 | tf_op jit(solution)/shard_map/dot_general | solution.py:184
  444.6 13.1 %add_convert_fusion = bf16[1024,2048]{1,0:T(8,128)(2,1)} fusion(f32[1024,2048]{1,0:T(8,128)} %fusion.54, bf16[2048,2048]{1,0:T(8,128)(2,1)} %param.10, s32[]{:T(128)S(6)} %select_n.82, bf16[1024,2048]{1,0:T(8,128)(2,1)} %all-gather.8.cloned.1.call-done, bf16[1024,1024]{1,0:T(8,128)(2,1)} %collective-permute-done.10, ...), kind=kOutput, calls=%fused_computation.27 | convolution fusion | flops 5379719168 | bytes 24124420 | tf_op jit(solution)/shard_map/dot_general | solution.py:184
  457.8 24.5 %fusion.7 = bf16[1024,4096]{1,0:T(8,128)(2,1)S(1)} fusion(bf16[1024,2048]{1,0:T(8,128)(2,1)} %add_convert_fusion, bf16[2048,4096]{1,0:T(8,128)(2,1)} %param.18), kind=kOutput, calls=%fused_computation.8 | convolution fusion | flops 17217617920 | bytes 29360128 | tf_op jit(solution)/shard_map/dot_general | solution.py:184
  482.3 3.3 copy-done.28
  485.7 8.0 %fusion.30 = f32[1024,512]{1,0:T(8,128)} fusion(bf16[1024,4096]{1,0:T(8,128)(2,1)S(1)} %fusion.7, bf16[4096,2048]{1,0:T(8,128)(2,1)} %param.19), kind=kOutput, calls=%fused_computation.34 | convolution fusion | flops 4294967296 | bytes 14680064 | tf_op jit(solution)/shard_map/dot_general | solution.py:184
  493.6 15.2 %fusion.15 = bf16[1024,2048]{1,0:T(8,128)(2,1)} fusion(bf16[1024,2048]{1,0:T(8,128)(2,1)} %add_convert_fusion, bf16[2048,2048]{1,0:T(8,128)(2,1)} %all-gather.10.cloned.1.call-done), kind=kOutput, calls=%fused_computation.18 | convolution fusion | flops 8608808960 | bytes 16777216 | tf_op jit(solution)/shard_map/dot_general | solution.py:184
  508.8 15.3 %fusion.23 = bf16[1024,2048]{1,0:T(8,128)(2,1)} fusion(bf16[1024,2048]{1,0:T(8,128)(2,1)} %add_convert_fusion, bf16[2048,2048]{1,0:T(8,128)(2,1)} %all-gather.14.cloned.1.call-done), kind=kOutput, calls=%fused_computation.26 | convolution fusion | flops 8608808960 | bytes 16777216 | tf_op jit(solution)/shard_map/dot_general | solution.py:184
  524.1 5.3 fusion.52
  529.5 5.3 broadcast_in_dim.44
  536.0 4.7 constant_dynamic-update-slice_fusion.1
  540.7 1.9 collective-permute-start.15
  542.6 10.4 %fusion.28 = f32[1024,512]{1,0:T(8,128)} fusion(bf16[1024,4096]{1,0:T(8,128)(2,1)} %copy-done.28, bf16[4096,2048]{1,0:T(8,128)(2,1)} %param.19), kind=kOutput, calls=%fused_computation.32 | convolution fusion | flops 4294967296 | bytes 14680064 | tf_op jit(solution)/shard_map/dot_general | solution.py:184
  553.0 5.3 fusion.48
  558.4 7.9 %collective-permute-done.15 = bf16[1024,512]{1,0:T(8,128)(2,1)S(1)} collective-permute-done((bf16[1024,512]{1,0:T(8,128)(2,1)S(1)}, bf16[1024,512]{1,0:T(8,128)(2,1)S(1)}, u32[]{:S(2)}, u32[]{:S(2)}) %collective-permute-start.15) | collective-permute-done | bytes 1048608 | tf_op jit(solution)/shard_map/ppermute | solution.py:178
  567.3 4.8 constant_dynamic-update-slice_fusion.5
  572.1 1.7 collective-permute-start.17
  573.8 8.2 %fusion.26 = f32[1024,512]{1,0:T(8,128)} fusion(bf16[1024,4096]{1,0:T(8,128)(2,1)S(1)} %bitcast.89, bf16[4096,2048]{1,0:T(8,128)(2,1)} %param.19), kind=kOutput, calls=%fused_computation.30 | convolution fusion | flops 4294967296 | bytes 14680064 | tf_op jit(solution)/shard_map/dot_general | solution.py:184
  582.1 5.3 fusion.44
  587.4 9.3 %collective-permute-done.17 = bf16[1024,512]{1,0:T(8,128)(2,1)S(1)} collective-permute-done((bf16[1024,512]{1,0:T(8,128)(2,1)S(1)}, bf16[1024,512]{1,0:T(8,128)(2,1)S(1)}, u32[]{:S(2)}, u32[]{:S(2)}) %collective-permute-start.17) | collective-permute-done | bytes 1048608 | tf_op jit(solution)/shard_map/ppermute | solution.py:178
  597.8 4.8 constant_dynamic-update-slice_fusion.7
  602.6 1.6 collective-permute-start.19
  604.2 8.0 %fusion.24 = f32[1024,512]{1,0:T(8,128)} fusion(bf16[1024,4096]{1,0:T(8,128)(2,1)S(1)} %bitcast.91, bf16[4096,2048]{1,0:T(8,128)(2,1)} %param.19), kind=kOutput, calls=%fused_computation.28 | convolution fusion | flops 4294967296 | bytes 14680064 | tf_op jit(solution)/shard_map/dot_general | solution.py:184
  612.2 5.3 fusion.40
  617.5 8.9 %collective-permute-done.19 = bf16[1024,512]{1,0:T(8,128)(2,1)S(1)} collective-permute-done((bf16[1024,512]{1,0:T(8,128)(2,1)S(1)}, bf16[1024,512]{1,0:T(8,128)(2,1)S(1)}, u32[]{:S(2)}, u32[]{:S(2)}) %collective-permute-start.19) | collective-permute-done | bytes 1048608 | tf_op jit(solution)/shard_map/ppermute | solution.py:178
  627.5 4.7 constant_dynamic-update-slice_fusion.3
  632.1 1.4 collective-permute-start.21
  633.6 21.5 %collective-permute-done.21 = bf16[1024,512]{1,0:T(8,128)(2,1)S(1)} collective-permute-done((bf16[1024,512]{1,0:T(8,128)(2,1)S(1)}, bf16[1024,512]{1,0:T(8,128)(2,1)S(1)}, u32[]{:S(2)}, u32[]{:S(2)}) %collective-permute-start.21) | collective-permute-done | bytes 1048608 | tf_op jit(solution)/shard_map/ppermute | solution.py:178
  (145 shorter events, 28.3 us)
Async XLA Ops:
  6.5 438.1 %all-gather.8.cloned.1.call-start = ((), (), s32[]{:S(2)}) async-start(), calls=%async_computation | async-start | bytes 5242880 | tf_op jit(solution)/shard_map/all_gather | solution.py:196
  7.9 26.5 %collective-permute-start.11 = (bf16[256,2048]{1,0:T(8,128)(2,1)S(1)}, bf16[256,2048]{1,0:T(8,128)(2,1)S(1)}, u32[]{:S(2)}, u32[]{:S(2)}) collective-permute-start(bf16[256,2048]{1,0:T(8,128)(2,1)S(1)} %constant_dynamic-slice_fusion.2), channel_id=1, source_target_pairs={{0,4},{4,0},{1,5},{5,1},{2,6},{6,2},{3,7},{7,3}} | collective-permute-start | bytes 3145736 | tf_op jit(solution)/shard_map/ppermute | solution.py:178
  34.4 1.0 copy-start.6
  35.4 458.3 %all-gather.10.cloned.1.call-start = ((), (), s32[]{:S(2)}) async-start(), calls=%async_computation.1 | async-start | bytes 10485760 | tf_op jit(solution)/shard_map/all_gather | solution.py:196
  39.5 46.8 %collective-permute-start.12 = (bf16[512,2048]{1,0:T(8,128)(2,1)S(1)}, bf16[512,2048]{1,0:T(8,128)(2,1)S(1)}, u32[]{:S(2)}, u32[]{:S(2)}) collective-permute-start(bf16[512,2048]{1,0:T(8,128)(2,1)S(1)} %get-tuple-element.17), channel_id=1, source_target_pairs={{0,4},{4,0},{1,5},{5,1},{2,6},{6,2},{3,7},{7,3}} | collective-permute-start | bytes 6291464 | tf_op jit(solution)/shard_map/ppermute | solution.py:178
  86.3 1.3 copy-start
  87.6 421.2 %all-gather.14.cloned.1.call-start = ((), (), s32[]{:S(2)}) async-start(), calls=%async_computation.3 | async-start | bytes 10485760 | tf_op jit(solution)/shard_map/all_gather | solution.py:196
  87.7 46.2 %collective-permute-start.14 = (bf16[512,2048]{1,0:T(8,128)(2,1)}, bf16[512,2048]{1,0:T(8,128)(2,1)S(1)}, u32[]{:S(2)}, u32[]{:S(2)}) collective-permute-start(bf16[512,2048]{1,0:T(8,128)(2,1)} %get-tuple-element.16), channel_id=1, source_target_pairs={{0,4},{4,0},{1,5},{5,1},{2,6},{6,2},{3,7},{7,3}} | collective-permute-start | bytes 6291464 | tf_op jit(solution)/shard_map/ppermute | solution.py:178
  133.8 1.3 copy-start.1
  135.2 389.0 %all-gather.12.cloned.1.call-start = ((), (), s32[]{:S(2)}) async-start(), calls=%async_computation.2 | async-start | bytes 5242880 | tf_op jit(solution)/shard_map/all_gather | solution.py:196
  135.2 28.6 %copy-start.11 = (s32[512]{0:T(512)S(1)}, s32[512]{0:T(512)}, u32[]{:S(2)}) copy-start(s32[512]{0:T(512)} %param.11) | copy-start | bytes 6148
  139.0 22.7 %collective-permute-start.13 = (bf16[1024,512]{1,0:T(8,128)(2,1)S(1)}, bf16[1024,512]{1,0:T(8,128)(2,1)S(1)}, u32[]{:S(2)}, u32[]{:S(2)}) collective-permute-start(bf16[1024,512]{1,0:T(8,128)(2,1)S(1)} %get-tuple-element.15), channel_id=1, source_target_pairs={{0,4},{4,0},{1,5},{5,1},{2,6},{6,2},{3,7},{7,3}} | collective-permute-start | bytes 3145736 | tf_op jit(solution)/shard_map/ppermute | solution.py:178
  161.7 1.1 copy-start.7
  162.8 390.2 %all-gather.16.cloned.1.call-start = ((), (), s32[]{:S(2)}) async-start(), calls=%async_computation.4 | async-start | bytes 5242880 | tf_op jit(solution)/shard_map/all_gather | solution.py:196
  162.9 23.3 %collective-permute-start.16 = (bf16[1024,512]{1,0:T(8,128)(2,1)}, bf16[1024,512]{1,0:T(8,128)(2,1)}, u32[]{:S(2)}, u32[]{:S(2)}) collective-permute-start(bf16[1024,512]{1,0:T(8,128)(2,1)} %get-tuple-element.14), channel_id=1, source_target_pairs={{0,4},{4,0},{1,5},{5,1},{2,6},{6,2},{3,7},{7,3}} | collective-permute-start | bytes 3145736 | tf_op jit(solution)/shard_map/ppermute | solution.py:178
  173.0 14.1 %collective-permute-start = (bf16[256,2048]{1,0:T(8,128)(2,1)}, bf16[256,2048]{1,0:T(8,128)(2,1)}, u32[]{:S(2)}, u32[]{:S(2)}) collective-permute-start(bf16[256,2048]{1,0:T(8,128)(2,1)} %constant_dynamic-slice_fusion.5), channel_id=1, source_target_pairs={{0,1},{1,0},{2,3},{3,2},{4,5},{5,4},{6,7},{7,6}} | collective-permute-start | bytes 3145736 | tf_op jit(solution)/shard_map/ppermute | solution.py:181
  186.1 395.9 %all-gather.18.cloned.1.call-start = ((), (), s32[]{:S(2)}) async-start(), calls=%async_computation.5 | async-start | bytes 5242880 | tf_op jit(solution)/shard_map/all_gather | solution.py:196
  186.2 49.0 %collective-permute-start.18 = (bf16[1024,512]{1,0:T(8,128)(2,1)}, bf16[1024,512]{1,0:T(8,128)(2,1)}, u32[]{:S(2)}, u32[]{:S(2)}) collective-permute-start(bf16[1024,512]{1,0:T(8,128)(2,1)} %get-tuple-element.13), channel_id=1, source_target_pairs={{0,4},{4,0},{1,5},{5,1},{2,6},{6,2},{3,7},{7,3}} | collective-permute-start | bytes 3145736 | tf_op jit(solution)/shard_map/ppermute | solution.py:178
  187.1 35.2 %slice-start = ((s8[8388608]{0:T(1024)(128)(4,1)}), s8[4194304]{0:T(1024)(128)(4,1)S(1)}, s32[]{:S(2)}) async-start(s8[8388608]{0:T(1024)(128)(4,1)} %bitcast.86), calls=%async_computation.7 | async-start | bytes 8388608
  188.9 33.5 %slice-start.1 = ((s8[8388608]{0:T(1024)(128)(4,1)}), s8[4194304]{0:T(1024)(128)(4,1)S(1)}, s32[]{:S(2)}) async-start(s8[8388608]{0:T(1024)(128)(4,1)} %bitcast.86), calls=%async_computation.8 | async-start | bytes 8388608
  188.9 33.5 %copy-start.14 = (bf16[2048,1024]{1,0:T(8,128)(2,1)S(1)}, bf16[2048,1024]{1,0:T(8,128)(2,1)}, u32[]{:S(2)}) copy-start(bf16[2048,1024]{1,0:T(8,128)(2,1)} %param.14) | copy-start | bytes 12582916
  188.9 33.0 %collective-permute-start.1 = (bf16[256,2048]{1,0:T(8,128)(2,1)S(1)}, bf16[256,2048]{1,0:T(8,128)(2,1)S(1)}, u32[]{:S(2)}, u32[]{:S(2)}) collective-permute-start(bf16[256,2048]{1,0:T(8,128)(2,1)S(1)} %dynamic-slice_add_fusion), channel_id=1, source_target_pairs={{0,2},{1,3},{2,0},{3,1},{4,6},{5,7},{6,4},{7,5}} | collective-permute-start | bytes 3145736 | tf_op jit(solution)/shard_map/ppermute | solution.py:181
  203.6 27.9 %copy-start.8 = (bf16[2048,1024]{1,0:T(8,128)(2,1)}, bf16[2048,1024]{1,0:T(8,128)(2,1)S(1)}, u32[]{:S(2)}) copy-start(bf16[2048,1024]{1,0:T(8,128)(2,1)S(1)} %convolution_convert_fusion.1.v_ref) | copy-start | bytes 12582916
  222.3 20.0 %collective-permute-start.2 = (bf16[256,2048]{1,0:T(8,128)(2,1)S(1)}, bf16[256,2048]{1,0:T(8,128)(2,1)}, u32[]{:S(2)}, u32[]{:S(2)}) collective-permute-start(bf16[256,2048]{1,0:T(8,128)(2,1)S(1)} %add.184), channel_id=1, source_target_pairs={{0,1},{1,0},{2,3},{3,2},{4,5},{5,4},{6,7},{7,6}} | collective-permute-start | bytes 3145736 | tf_op jit(solution)/shard_map/ppermute | solution.py:181
  231.5 2.4 copy-start.9
  233.9 59.3 %collective-permute-start.9 = (bf16[2,256,1024]{2,1,0:T(8,128)(2,1)}, bf16[2,256,1024]{2,1,0:T(8,128)(2,1)}, u32[]{:S(2)}, u32[]{:S(2)}) collective-permute-start(bf16[2,256,1024]{2,1,0:T(8,128)(2,1)} %pad_maximum_fusion.4), channel_id=1, source_target_pairs={{1,0},{2,1},{3,2},{5,4},{6,5},{7,6}} | collective-permute-start | bytes 3145736 | tf_op jit(solution)/shard_map/ppermute | solution.py:181
  235.2 377.0 %all-gather.20.cloned.1.call-start = ((), (), s32[]{:S(2)}) async-start(), calls=%async_computation.6 | async-start | bytes 5242880 | tf_op jit(solution)/shard_map/all_gather | solution.py:196
  236.4 59.2 %collective-permute-start.8 = (bf16[2,256,1024]{2,1,0:T(8,128)(2,1)}, bf16[2,256,1024]{2,1,0:T(8,128)(2,1)}, u32[]{:S(2)}, u32[]{:S(2)}) collective-permute-start(bf16[2,256,1024]{2,1,0:T(8,128)(2,1)} %pad_maximum_fusion.3), channel_id=1, source_target_pairs={{0,1},{1,2},{2,3},{4,5},{5,6},{6,7}} | collective-permute-start | bytes 3145736 | tf_op jit(solution)/shard_map/ppermute | solution.py:181
  240.8 52.3 %collective-permute-start.20 = (bf16[1024,512]{1,0:T(8,128)(2,1)S(1)}, bf16[1024,512]{1,0:T(8,128)(2,1)}, u32[]{:S(2)}, u32[]{:S(2)}) collective-permute-start(bf16[1024,512]{1,0:T(8,128)(2,1)S(1)} %get-tuple-element.12), channel_id=1, source_target_pairs={{0,4},{4,0},{1,5},{5,1},{2,6},{6,2},{3,7},{7,3}} | collective-permute-start | bytes 3145736 | tf_op jit(solution)/shard_map/ppermute | solution.py:178
  242.3 2.7 copy-start.12
  243.8 1.0 copy-start.4
  243.8 4.5 copy-start.2
  270.4 14.3 %copy-start.10 = (f32[8,513]{1,0:T(8,128)S(1)}, f32[8,513]{1,0:T(8,128)}, u32[]{:S(2)}) copy-start(f32[8,513]{1,0:T(8,128)} %param.12) | copy-start | bytes 49252
  270.5 16.0 %collective-permute-start.3 = (f32[256,1152]{1,0:T(8,128)S(1)}, f32[256,1152]{1,0:T(8,128)S(1)}, u32[]{:S(2)}, u32[]{:S(2)}) collective-permute-start(f32[256,1152]{1,0:T(8,128)S(1)} %constant_dynamic-slice_fusion.4), channel_id=1, source_target_pairs={{0,1},{1,0},{2,3},{3,2},{4,5},{5,4},{6,7},{7,6}} | collective-permute-start | bytes 3538952 | tf_op jit(solution)/shard_map/ppermute | solution.py:181
  292.2 28.7 %collective-permute-start.4 = (f32[128,1152]{1,0:T(8,128)S(1)}, f32[128,1152]{1,0:T(8,128)S(1)}, u32[]{:S(2)}, u32[]{:S(2)}) collective-permute-start(f32[128,1152]{1,0:T(8,128)S(1)} %constant_dynamic-slice_fusion.3), channel_id=1, source_target_pairs={{0,2},{1,3},{2,0},{3,1},{4,6},{5,7},{6,4},{7,5}} | collective-permute-start | bytes 1769480 | tf_op jit(solution)/shard_map/ppermute | solution.py:181
  293.1 29.6 %copy-start.3 = (bf16[256,2048]{1,0:T(8,128)(2,1)S(1)}, bf16[256,2048]{1,0:T(8,128)(2,1)}, u32[]{:S(2)}) copy-start(bf16[256,2048]{1,0:T(8,128)(2,1)} %copy-done.2) | copy-start | bytes 3145732
  293.1 29.6 %copy-start.5 = (bf16[256,2048]{1,0:T(8,128)(2,1)S(1)}, bf16[256,2048]{1,0:T(8,128)(2,1)}, u32[]{:S(2)}) copy-start(bf16[256,2048]{1,0:T(8,128)(2,1)} %copy-done.4) | copy-start | bytes 3145732
  293.2 29.6 %copy-start.13 = (bf16[2048,1024]{1,0:T(8,128)(2,1)S(1)}, bf16[2048,1024]{1,0:T(8,128)(2,1)}, u32[]{:S(2)}) copy-start(bf16[2048,1024]{1,0:T(8,128)(2,1)} %param.15) | copy-start | bytes 12582916
  322.0 8.5 %copy-start.15 = (bf16[2048,1024]{1,0:T(8,128)(2,1)S(1)}, bf16[2048,1024]{1,0:T(8,128)(2,1)}, u32[]{:S(2)}) copy-start(bf16[2048,1024]{1,0:T(8,128)(2,1)} %param.14) | copy-start | bytes 12582916
  322.1 8.0 %collective-permute-start.5 = (bf16[128,1024]{1,0:T(8,128)(2,1)S(1)}, bf16[128,1024]{1,0:T(8,128)(2,1)S(1)}, u32[]{:S(2)}, u32[]{:S(2)}) collective-permute-start(bf16[128,1024]{1,0:T(8,128)(2,1)S(1)} %fusion.92), channel_id=1, source_target_pairs={{0,4},{4,0},{1,5},{5,1},{2,6},{6,2},{3,7},{7,3}} | collective-permute-start | bytes 786440 | tf_op jit(solution)/shard_map/ppermute | solution.py:178
  330.1 21.0 %collective-permute-start.6 = (bf16[128,2048]{1,0:T(8,128)(2,1)S(1)}, bf16[128,2048]{1,0:T(8,128)(2,1)S(1)}, u32[]{:S(2)}, u32[]{:S(2)}) collective-permute-start(bf16[128,2048]{1,0:T(8,128)(2,1)S(1)} %pad_maximum_fusion.8), channel_id=1, source_target_pairs={{0,2},{1,3},{2,0},{3,1},{4,6},{5,7},{6,4},{7,5}} | collective-permute-start | bytes 1572872 | tf_op jit(solution)/shard_map/ppermute | solution.py:181
  351.1 80.2 %collective-permute-start.7 = (bf16[256,2048]{1,0:T(8,128)(2,1)S(1)}, bf16[256,2048]{1,0:T(8,128)(2,1)}, u32[]{:S(2)}, u32[]{:S(2)}) collective-permute-start(bf16[256,2048]{1,0:T(8,128)(2,1)S(1)} %pad_maximum_fusion.2), channel_id=1, source_target_pairs={{0,1},{1,0},{2,3},{3,2},{4,5},{5,4},{6,7},{7,6}} | collective-permute-start | bytes 3145736 | tf_op jit(solution)/shard_map/ppermute | solution.py:181
  388.4 56.3 %collective-permute-start.10 = (bf16[1024,1024]{1,0:T(8,128)(2,1)}, bf16[1024,1024]{1,0:T(8,128)(2,1)}, u32[]{:S(2)}, u32[]{:S(2)}) collective-permute-start(bf16[1024,1024]{1,0:T(8,128)(2,1)} %window_attention.5), channel_id=1, source_target_pairs={{0,4},{4,0},{1,5},{5,1},{2,6},{6,2},{3,7},{7,3}} | collective-permute-start | bytes 6291464 | tf_op jit(solution)/shard_map/ppermute | solution.py:178
  482.3 3.3 copy-start.28
  524.1 10.7 %copy-start.24 = (f32[1024,512]{1,0:T(8,128)S(1)}, f32[1024,512]{1,0:T(8,128)}, u32[]{:S(2)}) copy-start(f32[1024,512]{1,0:T(8,128)} %fusion.30) | copy-start | bytes 6291460
  529.5 5.3 copy-start.16
  529.5 6.5 copy-start.20
  540.7 25.5 %collective-permute-start.15 = (bf16[1024,512]{1,0:T(8,128)(2,1)S(1)}, bf16[1024,512]{1,0:T(8,128)(2,1)S(1)}, u32[]{:S(2)}, u32[]{:S(2)}) collective-permute-start(bf16[1024,512]{1,0:T(8,128)(2,1)S(1)} %get-tuple-element.33), channel_id=1, source_target_pairs={{0,4},{4,0},{1,5},{5,1},{2,6},{6,2},{3,7},{7,3}} | collective-permute-start | bytes 3145736 | tf_op jit(solution)/shard_map/ppermute | solution.py:178
  553.0 14.3 %copy-start.17 = (bf16[4096,512]{1,0:T(8,128)(2,1)S(1)}, bf16[4096,512]{1,0:T(8,128)(2,1)}, u32[]{:S(2)}) copy-start(bf16[4096,512]{1,0:T(8,128)(2,1)} %all-gather.16.cloned.1.call-done) | copy-start | bytes 12582916
  553.0 14.3 %copy-start.21 = (bf16[1024,2048]{1,0:T(8,128)(2,1)S(1)}, bf16[1024,2048]{1,0:T(8,128)(2,1)}, u32[]{:S(2)}) copy-start(bf16[1024,2048]{1,0:T(8,128)(2,1)} %fusion.23) | copy-start | bytes 12582916
  553.0 14.3 %copy-start.26 = (f32[1024,512]{1,0:T(8,128)S(1)}, f32[1024,512]{1,0:T(8,128)}, u32[]{:S(2)}) copy-start(f32[1024,512]{1,0:T(8,128)} %fusion.28) | copy-start | bytes 6291460
  553.0 20.8 %slice-start.2 = ((s8[8388608]{0:T(1024)(128)(4,1)}), s8[4194304]{0:T(1024)(128)(4,1)S(1)}, s32[]{:S(2)}) async-start(s8[8388608]{0:T(1024)(128)(4,1)} %bitcast.88), calls=%async_computation.9 | async-start | bytes 8388608
  567.3 6.6 slice-start.3
  572.1 24.7 %collective-permute-start.17 = (bf16[1024,512]{1,0:T(8,128)(2,1)S(1)}, bf16[1024,512]{1,0:T(8,128)(2,1)S(1)}, u32[]{:S(2)}, u32[]{:S(2)}) collective-permute-start(bf16[1024,512]{1,0:T(8,128)(2,1)S(1)} %get-tuple-element.35), channel_id=1, source_target_pairs={{0,4},{4,0},{1,5},{5,1},{2,6},{6,2},{3,7},{7,3}} | collective-permute-start | bytes 3145736 | tf_op jit(solution)/shard_map/ppermute | solution.py:178
  582.1 15.7 %copy-start.18 = (bf16[4096,512]{1,0:T(8,128)(2,1)S(1)}, bf16[4096,512]{1,0:T(8,128)(2,1)}, u32[]{:S(2)}) copy-start(bf16[4096,512]{1,0:T(8,128)(2,1)} %all-gather.18.cloned.1.call-done) | copy-start | bytes 12582916
  582.1 15.7 %copy-start.22 = (bf16[1024,2048]{1,0:T(8,128)(2,1)S(1)}, bf16[1024,2048]{1,0:T(8,128)(2,1)}, u32[]{:S(2)}) copy-start(bf16[1024,2048]{1,0:T(8,128)(2,1)} %fusion.23) | copy-start | bytes 12582916
  582.1 15.7 %copy-start.27 = (f32[1024,512]{1,0:T(8,128)S(1)}, f32[1024,512]{1,0:T(8,128)}, u32[]{:S(2)}) copy-start(f32[1024,512]{1,0:T(8,128)} %fusion.26) | copy-start | bytes 6291460
  582.1 22.1 %slice-start.4 = ((s8[8388608]{0:T(1024)(128)(4,1)}), s8[4194304]{0:T(1024)(128)(4,1)S(1)}, s32[]{:S(2)}) async-start(s8[8388608]{0:T(1024)(128)(4,1)} %bitcast.90), calls=%async_computation.11 | async-start | bytes 8388608
  597.8 6.4 slice-start.5
  602.6 23.8 %collective-permute-start.19 = (bf16[1024,512]{1,0:T(8,128)(2,1)S(1)}, bf16[1024,512]{1,0:T(8,128)(2,1)S(1)}, u32[]{:S(2)}, u32[]{:S(2)}) collective-permute-start(bf16[1024,512]{1,0:T(8,128)(2,1)S(1)} %get-tuple-element.37), channel_id=1, source_target_pairs={{0,4},{4,0},{1,5},{5,1},{2,6},{6,2},{3,7},{7,3}} | collective-permute-start | bytes 3145736 | tf_op jit(solution)/shard_map/ppermute | solution.py:178
  612.2 15.3 %copy-start.19 = (bf16[4096,512]{1,0:T(8,128)(2,1)S(1)}, bf16[4096,512]{1,0:T(8,128)(2,1)}, u32[]{:S(2)}) copy-start(bf16[4096,512]{1,0:T(8,128)(2,1)} %all-gather.20.cloned.1.call-done) | copy-start | bytes 12582916
  612.2 15.3 %copy-start.23 = (bf16[1024,2048]{1,0:T(8,128)(2,1)S(1)}, bf16[1024,2048]{1,0:T(8,128)(2,1)}, u32[]{:S(2)}) copy-start(bf16[1024,2048]{1,0:T(8,128)(2,1)} %fusion.23) | copy-start | bytes 12582916
  612.2 15.3 %copy-start.25 = (f32[1024,512]{1,0:T(8,128)S(1)}, f32[1024,512]{1,0:T(8,128)}, u32[]{:S(2)}) copy-start(f32[1024,512]{1,0:T(8,128)} %fusion.24) | copy-start | bytes 6291460
  632.1 22.9 %collective-permute-start.21 = (bf16[1024,512]{1,0:T(8,128)(2,1)S(1)}, bf16[1024,512]{1,0:T(8,128)(2,1)S(1)}, u32[]{:S(2)}, u32[]{:S(2)}) collective-permute-start(bf16[1024,512]{1,0:T(8,128)(2,1)S(1)} %get-tuple-element.39), channel_id=1, source_target_pairs={{0,4},{4,0},{1,5},{5,1},{2,6},{6,2},{3,7},{7,3}} | collective-permute-start | bytes 3145736 | tf_op jit(solution)/shard_map/ppermute | solution.py:178
Sparse Core Ops, SparseCore 0:
  35.5 32.8 all-gather.7
  87.7 56.3 all-gather.9
  145.7 67.1 all-gather.13
  214.3 34.2 all-gather.11
  250.0 31.6 all-gather.15
  283.1 44.3 all-gather.17
  329.0 37.9 all-gather.19
